TPU v7x, 512 devices: a 4x2x32 block of a 4x8x32 slice. The times are simulated.
512 devices in a mesh: crops: 2 (over y), dap: 64 (over z, core), chan: 4 (over x).
Axes of the slice: x: 4, y: 2, z: 32, core: 2. Of those that a mesh axis runs over, the one named last changes fastest.
The devices are a block of a 4x8x32 slice.
Arguments:
- prior_pair: bfloat16 [512, 256, 128], P(('crops', 'dap')), parts along dimension 0, may hold values from -12 to 12
- single: bfloat16 [512, 384], P(('crops', 'dap')), parts along dimension 0, may hold values from -6 to 6
- target: int32 [512], P(('crops', 'dap')), parts along dimension 0, may hold values from 0 to 21
- residue_mask: int32 [512], P(('crops', 'dap')), parts along dimension 0, may hold values 0 or 1
- recycle_gain: float32 [128], replicated, may hold values from 0.5 to 1.5
- recycle_bias: float32 [128], replicated, may hold values from -3 to 3
- left_single: bfloat16 [384, 128], replicated, may hold values from -0.3125 to 0.3125
- right_single: bfloat16 [384, 128], replicated, may hold values from -0.3125 to 0.3125
- left_target: bfloat16 [22, 128], replicated, may hold values from -3 to 3
- right_target: bfloat16 [22, 128], replicated, may hold values from -3 to 3
- tri_gain: float32 [2, 128], replicated, may hold values from 0.25 to 1.75
- tri_proj: bfloat16 [2, 128, 4, 128], replicated, may hold values from -0.5 to 0.5
- tri_gate: bfloat16 [2, 128, 128], replicated, may hold values from -0.5 to 0.5
- tri_gate_bias: float32 [2, 128], replicated, may hold values from -4 to 4
- tri_out_gain: float32 [2, 128], replicated, may hold values from 0.25 to 1.75
- tri_out: bfloat16 [2, 128, 128], replicated, may hold values from -0.5 to 0.5
Outputs:
- updated_pair: bfloat16 [512, 256, 128], P(('crops', 'dap')), parts along dimension 0
There are 2 independent parts, one for each index of `crops`. A program takes and returns all parts, laid end to end along the dimension named above; an argument that names none is the same for every part. Nothing has to cross between parts.
All inputs are finite; a program needn't handle non-finite values. No bound on the sum of `residue_mask` on one device may be relied on, other than what follows from the above.
Results may differ from a plain program's by a relative error of at most 0.0085.
Values may be sent and summed in bfloat16 or wider, within the bound.
A program may use at most 64 MiB of HBM per device.

v0:
```python
import math

import jax
import jax.numpy as jnp
from jax import lax
from jax.sharding import PartitionSpec as P


def side_by_side(arrays, axis, dim, along):
    widths = [math.prod(a.shape[along:]) for a in arrays]
    both = jnp.concatenate(
        [a.reshape(*a.shape[:along], w) for a, w in zip(arrays, widths)], axis=along
    )
    out = lax.all_gather(both, axis, axis=dim, tiled=True)
    blocks = jnp.split(out, [sum(widths[:k]) for k in range(1, len(widths))], axis=along)
    return tuple((b.reshape(*out.shape[:along], *a.shape[along:]) for a, b in zip(arrays, blocks)))


def in_order(blocks, dim):
    lengths = list(blocks.shape[1:])
    lengths[dim] *= blocks.shape[0]
    return jnp.moveaxis(blocks, 0, dim).reshape(lengths)


def copy_for_each(shard, axis):
    peers = lax.axis_size(axis)
    return lax.all_to_all(
        jnp.broadcast_to(shard[None], (peers, *shard.shape)), axis, 0, 0, tiled=True
    )


def gathered_copies(shard, axis, dim):
    return in_order(copy_for_each(shard, axis), dim)


def layer_norm(values, axis):
    center = values - jnp.mean(values, axis=axis, keepdims=True)
    spread = jnp.mean(center * center, axis=axis, keepdims=True)
    return center * lax.rsqrt(spread + 1e-05)


def gated_edges(projected, mask_block):
    masked = mask_block[:, :, None]
    first = (masked * jax.nn.sigmoid(projected[:, :, 1]) * projected[:, :, 0]).astype(jnp.bfloat16)
    second = (masked * jax.nn.sigmoid(projected[:, :, 3]) * projected[:, :, 2]).astype(jnp.bfloat16)
    return (jnp.transpose(first, (2, 0, 1)), jnp.transpose(second, (2, 0, 1)))


def body(
    prior_pair,
    single,
    target,
    residue_mask,
    recycle_gain,
    recycle_bias,
    left_single,
    right_single,
    left_target,
    right_target,
    tri_gain,
    tri_proj,
    tri_gate,
    tri_gate_bias,
    tri_out_gain,
    tri_out,
):
    row_count, col_count, depth = prior_pair.shape
    hidden_width = tri_proj.shape[3]
    mask_float = residue_mask.astype(jnp.float32)
    one_hot = (
        target[:, None] == jnp.arange(left_target.shape[0], dtype=jnp.int32)[None, :]
    ).astype(jnp.bfloat16)
    left_terms = jnp.dot(single, left_single, preferred_element_type=jnp.float32) + jnp.dot(
        one_hot, left_target, preferred_element_type=jnp.float32
    )
    right_terms = jnp.dot(single, right_single, preferred_element_type=jnp.float32) + jnp.dot(
        one_hot, right_target, preferred_element_type=jnp.float32
    )
    right_whole, mask_whole = side_by_side((right_terms, mask_float), "dap", 0, 1)
    pair_mask = mask_float[:, None] * mask_whole[None, :]
    prior_norm = layer_norm(prior_pair.astype(jnp.float32), 2) * recycle_gain + recycle_bias
    pair_state = (prior_norm + left_terms[:, None, :] + right_whole[None, :, :]).astype(
        jnp.bfloat16
    )
    groups = lax.axis_size("chan")
    member = lax.axis_index("chan")
    local_width = hidden_width // groups

    def local_edges(flat_normed, weights):
        weights_local = lax.dynamic_slice_in_dim(weights, member * local_width, local_width, 2)
        projected = jnp.dot(
            flat_normed,
            weights_local.reshape(depth, 4 * local_width),
            preferred_element_type=jnp.float32,
        )
        return gated_edges(projected.reshape(row_count, col_count, 4, local_width), pair_mask)

    for layer in range(2):
        normed = (layer_norm(pair_state.astype(jnp.float32), 2) * tri_gain[layer]).astype(
            jnp.bfloat16
        )
        flat_normed = normed.reshape(-1, depth)
        if layer == 0:
            outgoing_left_edges, outgoing_right_edges = local_edges(flat_normed, tri_proj[layer])
            product = jnp.einsum(
                "cik,cjk->cij",
                outgoing_left_edges,
                lax.all_gather(outgoing_right_edges, "dap", axis=1, tiled=True),
                preferred_element_type=jnp.float32,
            )
        else:
            left_edges, right_edges = local_edges(flat_normed, tri_proj[layer])
            transposed = lax.all_to_all(left_edges, "dap", split_axis=2, concat_axis=1, tiled=True)
            product = jnp.einsum(
                "cki,ckj->cij",
                transposed,
                lax.all_gather(right_edges, "dap", axis=1, tiled=True),
                preferred_element_type=jnp.float32,
            )
        full_product = gathered_copies(product.astype(jnp.bfloat16), "chan", 0)
        normed_hidden = (
            layer_norm(full_product.astype(jnp.float32), 0) * tri_out_gain[layer][:, None, None]
        ).astype(jnp.bfloat16)
        update = jnp.einsum(
            "cij,cd->ijd", normed_hidden, tri_out[layer], preferred_element_type=jnp.float32
        )
        gating = jax.nn.sigmoid(
            jnp.dot(flat_normed, tri_gate[layer], preferred_element_type=jnp.float32)
            + tri_gate_bias[layer]
        )
        pair_state = (
            pair_state.astype(jnp.float32) + gating.reshape(row_count, col_count, depth) * update
        ).astype(jnp.bfloat16)
    return pair_state


def solution(mesh):
    placed = (
        P(("crops", "dap"), None, None),
        P(("crops", "dap"), None),
        P(("crops", "dap")),
        P(("crops", "dap")),
        P(),
        P(),
        P(),
        P(),
        P(),
        P(),
        P(),
        P(),
        P(),
        P(),
        P(),
        P(),
    )
    return jax.shard_map(
        body, mesh=mesh, in_specs=placed, out_specs=P(("crops", "dap"), None, None), check_vma=False
    )
```

profile of v0, /device:TPU:33, one launch (start us, length us, event | category | flops | bytes accessed | tf_op | source)
XLA Modules:
  0.0 407.9 jit_solution(16664484103935328032)
XLA Ops:
  7.4 0.8 fusion.102
  8.3 0.9 convolution_add_fusion.2
  9.2 97.4 %all-gather = f32[64,4,129]{2,1,0:T(4,128)S(1)} all-gather(f32[1,4,129]{2,1,0:T(4,128)S(1)} %maximum_bitcast_fusion), channel_id=1, replica_groups=mesh['crops'=2,'dap'=64,'chan'=4] {'dap'}, dimensions={0}, use_global_device_ids=true | all-gather | bytes 134160 | tf_op jit(solution)/shard_map/all_gather | solution.py:14
  106.8 1.1 convert_reduce_fusion.3
  107.9 1.3 fusion.40
  109.2 1.0 fusion.101
  110.3 0.9 convolution_add_fusion.3
  111.2 1.5 convert_reduce_fusion
  113.1 0.8 slice_bitcast_fusion.7
  113.8 1.1 fusion.98
  116.9 121.3 %all-gather.4.cloned.1.call-done = bf16[32,256,256]{2,0,1:T(8,128)(2,1)} async-done(((bf16[32,4,256]{2,0,1:T(8,128)(2,1)}), bf16[32,256,256]{2,0,1:T(8,128)(2,1)}) %all-gather.4.cloned.1.call-update) | async-done | bytes 4194320 | tf_op jit(solution)/shard_map/all_gather | solution.py:108
  238.2 4.5 %fusion.17 = bf16[32,4,256]{2,1,0:T(4,128)(2,1)S(1)} fusion(bf16[32,256,256]{2,0,1:T(8,128)(2,1)} %all-gather.4.cloned.1.call-done, bf16[32,4,256]{2,0,1:T(8,128)(2,1)S(1)} %get-tuple-element.11), kind=kOutput, calls=%fused_computation.21 | convolution fusion | flops 16809984 | bytes 4325376 | tf_op jit(solution)/shard_map/cik,cjk->cij/dot_general | solution.py:105
  242.8 0.7 broadcast_in_dim.4
  243.5 4.0 all-to-all-start
  247.8 5.6 %all-to-all-done = bf16[4,32,4,256]{3,1,2,0:T(8,128)(2,1)S(1)} async-done(((bf16[4,32,4,256]{3,1,2,0:T(8,128)(2,1)}), bf16[4,32,4,256]{3,1,2,0:T(8,128)(2,1)S(1)}, u32[]{:S(2)}, u32[]{:S(2)}) %all-to-all-start) | async-done | bytes 262176 | tf_op jit(solution)/shard_map/all_to_all | solution.py:27
  256.0 0.8 reshape.193
  256.8 14.6 %all-to-all-start.1 = ((bf16[64,2,256]{2,1,0:T(2,128)(2,1)}), bf16[64,2,256]{2,1,0:T(2,128)(2,1)S(1)}, u32[]{:S(2)}, u32[]{:S(2)}) async-start(bf16[64,2,256]{2,1,0:T(2,128)(2,1)} %reshape.193), calls=%async_computation.1 | async-start | bytes 131072 | tf_op jit(solution)/shard_map/all_to_all | solution.py:113
  271.6 24.9 %all-to-all-done.1 = bf16[64,2,256]{2,1,0:T(2,128)(2,1)S(1)} async-done(((bf16[64,2,256]{2,1,0:T(2,128)(2,1)}), bf16[64,2,256]{2,1,0:T(2,128)(2,1)S(1)}, u32[]{:S(2)}, u32[]{:S(2)}) %all-to-all-start.1) | async-done | bytes 65568 | tf_op jit(solution)/shard_map/all_to_all | solution.py:113
  297.1 87.5 %all-gather.6.cloned.1.call-done = bf16[32,256,256]{2,0,1:T(8,128)(2,1)} async-done(((bf16[32,4,256]{2,0,1:T(8,128)(2,1)}), bf16[32,256,256]{2,0,1:T(8,128)(2,1)}) %all-gather.6.cloned.1.call-update) | async-done | bytes 4194320 | tf_op jit(solution)/shard_map/all_gather | solution.py:117
  384.6 4.5 %fusion.20 = bf16[32,4,256]{2,1,0:T(4,128)(2,1)S(1)} fusion(bf16[32,256,4]{1,2,0:T(4,128)(2,1)S(1)} %copy.69, bf16[32,256,256]{2,0,1:T(8,128)(2,1)} %all-gather.6.cloned.1.call-done), kind=kOutput, calls=%fused_computation.22 | convolution fusion | flops 16809984 | bytes 4325376 | tf_op jit(solution)/shard_map/cki,ckj->cij/dot_general | solution.py:114
  389.1 0.7 broadcast_in_dim.5
  389.9 4.1 all-to-all-start.2
  394.2 5.6 %all-to-all-done.2 = bf16[4,32,4,256]{3,1,2,0:T(8,128)(2,1)S(1)} async-done(((bf16[4,32,4,256]{3,1,2,0:T(8,128)(2,1)}), bf16[4,32,4,256]{3,1,2,0:T(8,128)(2,1)S(1)}, u32[]{:S(2)}, u32[]{:S(2)}) %all-to-all-start.2) | async-done | bytes 262176 | tf_op jit(solution)/shard_map/all_to_all | solution.py:27
  400.1 1.0 fusion.14
  (62 shorter events, 7.5 us)
Async XLA Ops:
  6.5 0.9 copy-start
  6.6 110.1 %copy-start.2 = (f32[2,128]{1,0:T(2,128)S(1)}, f32[2,128]{1,0:T(2,128)}, u32[]{:S(2)}) copy-start(f32[2,128]{1,0:T(2,128)} %param.30) | copy-start | bytes 3076
  6.6 110.3 %copy-start.3 = (f32[2,128]{1,0:T(2,128)S(1)}, f32[2,128]{1,0:T(2,128)}, u32[]{:S(2)}) copy-start(f32[2,128]{1,0:T(2,128)} %param.29) | copy-start | bytes 3076
  6.6 231.6 %all-gather.4.cloned.1.call-start = ((), (), s32[]{:S(2)}) async-start(), calls=%async_computation.3 | async-start | bytes 4259840 | tf_op jit(solution)/shard_map/all_gather | solution.py:108
  114.9 132.6 %copy-start.4 = (bf16[2,128,128]{2,1,0:T(8,128)(2,1)S(1)}, bf16[2,128,128]{2,1,0:T(8,128)(2,1)}, u32[]{:S(2)}) copy-start(bf16[2,128,128]{2,1,0:T(8,128)(2,1)} %param.28) | copy-start | bytes 196612
  238.2 15.5 %copy-start.1 = (bf16[2,128,128]{2,1,0:T(8,128)(2,1)S(1)}, bf16[2,128,128]{2,1,0:T(8,128)(2,1)}, u32[]{:S(2)}) copy-start(bf16[2,128,128]{2,1,0:T(8,128)(2,1)} %param.31) | copy-start | bytes 196612
  243.5 9.9 %all-to-all-start = ((bf16[4,32,4,256]{3,1,2,0:T(8,128)(2,1)}), bf16[4,32,4,256]{3,1,2,0:T(8,128)(2,1)S(1)}, u32[]{:S(2)}, u32[]{:S(2)}) async-start(bf16[4,32,4,256]{3,1,2,0:T(8,128)(2,1)} %broadcast_in_dim.4), calls=%async_computation | async-start | bytes 524288 | tf_op jit(solution)/shard_map/all_to_all | solution.py:27
  247.5 137.1 %all-gather.6.cloned.1.call-start = ((), (), s32[]{:S(2)}) async-start(), calls=%async_computation.4 | async-start | bytes 4259840 | tf_op jit(solution)/shard_map/all_gather | solution.py:117
  256.8 39.6 %all-to-all-start.1 = ((bf16[64,2,256]{2,1,0:T(2,128)(2,1)}), bf16[64,2,256]{2,1,0:T(2,128)(2,1)S(1)}, u32[]{:S(2)}, u32[]{:S(2)}) async-start(bf16[64,2,256]{2,1,0:T(2,128)(2,1)} %reshape.193), calls=%async_computation.1 | async-start | bytes 131072 | tf_op jit(solution)/shard_map/all_to_all | solution.py:113
  389.9 10.0 %all-to-all-start.2 = ((bf16[4,32,4,256]{3,1,2,0:T(8,128)(2,1)}), bf16[4,32,4,256]{3,1,2,0:T(8,128)(2,1)S(1)}, u32[]{:S(2)}, u32[]{:S(2)}) async-start(bf16[4,32,4,256]{3,1,2,0:T(8,128)(2,1)} %broadcast_in_dim.5), calls=%async_computation.2 | async-start | bytes 524288 | tf_op jit(solution)/shard_map/all_to_all | solution.py:27
Sparse Core Ops, SparseCore 0:
  116.8 121.3 all-gather.3
  255.9 128.6 all-gather.5
where the time goes:
time: 409 us; the launch traced here: 408 us
  waiting for transfers between devices  245 us (60%)
  blocking collectives  97.4 us (24%)
  starting transfers between devices  22.7 us (6%)
  matrix products  15.1 us (4%)
  between operations  13.7 us (3%)
  other arithmetic  8.15 us (2%)
  local copies, waits for them, and re-layouts  5.89 us (1%)
    all_gather x1, waiting for transfers between devices, body(): lax.all_gather(outgoing_right_edges, 'dap', axis=1, tiled=True)  121 us
    all_gather x1, blocking collectives, side_by_side(): out = lax.all_gather(both, axis, axis=dim, tiled=True)  97.4 us
    all_gather x1, waiting for transfers between devices, body(): lax.all_gather(right_edges, 'dap', axis=1, tiled=True)  87.5 us
    all_to_all x1, waiting for transfers between devices, body(): lax.all_to_all(left_edges, 'dap', split_axis=2, concat_axis=1, tiled=True)  24.9 us
    all_to_all x1, starting transfers between devices, body(): lax.all_to_all(left_edges, 'dap', split_axis=2, concat_axis=1, tiled=True)  14.6 us
    all_to_all x2, waiting for transfers between devices, copy_for_each(): lax.all_to_all(jnp.broadcast_to(shard[None], (peers, *shard.shape)), axis...  11.2 us
  transfers between devices with their start and end apart: 5, of which 5 were waited for; matrix products, arithmetic and copies ran while one was open for 1% of the time, Pallas kernels for 0%

commit v1 on v0

v1 whole, which is shorter than its diff:
```python
import functools

import jax
import jax.numpy as jnp
from jax import lax
from jax.experimental import pallas as pl
from jax.experimental.pallas import tpu as pltpu
from jax.sharding import PartitionSpec as P

F32 = jnp.float32
BF16 = jnp.bfloat16
MESH = pl.DeviceIdType.MESH
EPS = 1e-05
LANES = 128


def selection(shape, column_of_row):
    rows = lax.broadcasted_iota(jnp.int32, shape, 0)
    columns = lax.broadcasted_iota(jnp.int32, shape, 1)
    return jnp.where(columns == column_of_row(rows), 1.0, 0.0).astype(BF16)


def nn(a, b):
    return lax.dot_general(a, b, (((1,), (0,)), ((), ())), preferred_element_type=F32)


def nt(a, b):
    return lax.dot_general(a, b, (((1,), (1,)), ((), ())), preferred_element_type=F32)


def norm_rows(values):
    scale = 1.0 / values.shape[0]
    center = values - jnp.sum(values, axis=0, keepdims=True) * scale
    spread = jnp.sum(center * center, axis=0, keepdims=True) * scale
    return center * lax.rsqrt(spread + EPS)


def column(row_vector):
    return jnp.transpose(jnp.broadcast_to(row_vector, (LANES, LANES)))


def kernel(
    rings,
    lanes_x,
    prior_ref,
    single_ref,
    target_ref,
    mask_ref,
    recycle_gain_ref,
    recycle_bias_ref,
    left_single_ref,
    right_single_ref,
    left_target_ref,
    right_target_ref,
    tri_gain_ref,
    tri_proj_ref,
    tri_gate_ref,
    tri_gate_bias_ref,
    tri_out_gain_ref,
    tri_out_ref,
    out_ref,
    terms,
    edges_out,
    left_in,
    right_in,
    product_out,
    product_in,
    base,
    pair,
    normed,
    weights,
    gate_weights,
    out_weights,
    columns,
    perm,
    perm_back,
    pick,
    pick_right,
    pick_left,
    terms_send,
    terms_recv,
    edge_send,
    edge_recv,
    back_send,
    back_recv,
    twin_send,
    twin_recv,
    lane_send,
    lane_recv,
):
    rows, cols, depth = prior_ref.shape
    blocks = rows * cols // LANES
    per_row = cols // LANES
    width = depth // lanes_x
    dap = lax.axis_index("dap")
    x = lax.axis_index("chan")
    z = dap // 2
    h = lax.rem(dap, 2)
    twin = {"dap": dap + 1 - 2 * h}

    def z_peer(t):
        up = (t + 1) // 2
        offset = rings // 2 + up * (1 - 2 * lax.rem(t + 1, 2))
        return lax.rem(z + offset, rings)

    def to_z(peer):
        return {"dap": 2 * peer + h}

    def to_x(t):
        return lax.rem(x + t, lanes_x)

    barrier = pltpu.get_barrier_semaphore()

    def greet(t, carry):
        pl.semaphore_signal(barrier, inc=1, device_id=to_z(z_peer(t)), device_id_type=MESH)
        return carry

    lax.fori_loop(0, rings - 1, greet, 0)
    pl.semaphore_signal(barrier, inc=1, device_id=twin, device_id_type=MESH)
    for t in range(1, lanes_x):
        pl.semaphore_signal(barrier, inc=1, device_id={"chan": to_x(t)}, device_id_type=MESH)

    single = single_ref[...]
    mask_of = [mask_ref[r].astype(F32) for r in range(rows)]

    def row_terms(weight_ref, table_ref):
        linear = nn(single, weight_ref[...])
        table = table_ref[...].astype(F32)
        classes = lax.broadcasted_iota(jnp.int32, table.shape, 0)
        picked = [
            jnp.sum(jnp.where(classes == target_ref[r], table, 0.0), axis=0, keepdims=True)
            for r in range(rows)
        ]
        return [linear[r : r + 1] + picked[r] for r in range(rows)]

    right_rows = row_terms(right_single_ref, right_target_ref)
    mask_rows = [jnp.full((1, depth), mask_of[r], F32) for r in range(rows)]
    tile = jnp.concatenate(right_rows + mask_rows, axis=0)
    terms[h, z] = jnp.where(h == 0, tile, pltpu.roll(tile, rows, 0))

    left_rows = row_terms(left_single_ref, left_target_ref)
    gain = recycle_gain_ref[...]
    bias = recycle_bias_ref[...]
    for r in range(rows):
        for jh in range(per_row):
            block = prior_ref[r, jh * LANES : (jh + 1) * LANES, :].astype(F32)
            center = block - jnp.mean(block, axis=1, keepdims=True)
            spread = jnp.mean(center * center, axis=1, keepdims=True)
            value = center * lax.rsqrt(spread + EPS) * gain + bias + left_rows[r]
            base[r * per_row + jh] = jnp.transpose(value)
    for u in range(2):
        for g in range(4):
            whole = tri_proj_ref[u, :, g * depth : (g + 1) * depth].astype(F32)
            weights[u, g] = jnp.transpose(whole).astype(BF16)
        gate_weights[u] = jnp.transpose(tri_gate_ref[u].astype(F32)).astype(BF16)
        out_weights[u] = jnp.transpose(tri_out_ref[u].astype(F32)).astype(BF16)
        columns[u, 0] = column(tri_gain_ref[u : u + 1, :])
        columns[u, 1] = column(tri_gate_bias_ref[u : u + 1, :])
        columns[u, 2] = column(tri_out_gain_ref[u : u + 1, :])
    size = rings * blocks
    perm[...] = selection((size, size), lambda q: lax.rem(q, blocks) * rings + q // blocks)
    perm_back[...] = selection((size, size), lambda q: lax.rem(q, rings) * blocks + q // rings)
    for half in range(2):
        pick[half] = selection((size, size), lambda q: q - lax.rem(q, 2) + half)
        pick_right[half] = selection(
            (size, 2 * size),
            lambda j: lax.rem(j // rows, 2) * size
            + (j // (2 * rows)) * blocks
            + 2 * lax.rem(j, rows)
            + half,
        )
    pick_left[...] = selection(
        (size, cols), lambda q: (q // blocks) * 2 * rows + rows * h + lax.rem(q, blocks) // 2
    )

    pl.semaphore_wait(barrier, rings - 1 + 1 + lanes_x - 1)

    def all_send(source, target, send, recv):
        def step(t, carry):
            peer = z_peer(t)
            pltpu.make_async_remote_copy(
                src_ref=source(peer),
                dst_ref=target(z),
                send_sem=send.at[peer],
                recv_sem=recv.at[z],
                device_id=to_z(peer),
                device_id_type=MESH,
            ).start()
            return carry

        lax.fori_loop(0, rings - 1, step, 0)

    def all_wait(source, target, send, recv, sent):
        def step(t, carry):
            peer = z_peer(rings - 2 - t)
            copy = pltpu.make_async_remote_copy(
                src_ref=source(peer),
                dst_ref=target(peer),
                send_sem=send.at[peer],
                recv_sem=recv.at[peer],
                device_id=to_z(peer),
                device_id_type=MESH,
            )
            if sent:
                copy.wait_send()
            else:
                copy.wait_recv()
            return carry

        lax.fori_loop(0, rings - 1, step, 0)

    def swap(buffer, k):
        def copy(parity):
            return pltpu.make_async_remote_copy(
                src_ref=buffer.at[parity],
                dst_ref=buffer.at[parity],
                send_sem=twin_send.at[k],
                recv_sem=twin_recv.at[k],
                device_id=twin,
                device_id_type=MESH,
            )

        copy(h).start()
        return copy(h), copy(1 - h)

    closing = []

    own_terms = lambda peer: terms.at[h, z]
    their_terms = lambda peer: terms.at[h, peer]
    all_send(own_terms, their_terms, terms_send, terms_recv)
    all_wait(own_terms, their_terms, terms_send, terms_recv, False)
    closing.append(functools.partial(all_wait, own_terms, their_terms, terms_send, terms_recv, True))
    sent, got = swap(terms, 0)
    got.wait_recv()
    closing.append(sent.wait_send)
    first, second = terms[0], terms[1]
    upper = lax.broadcasted_iota(jnp.int32, first.shape, 1) < rows
    right_whole = jnp.where(upper, first, second).reshape(cols, depth)
    mask_whole = jnp.where(upper, second, first)
    mask_whole = pltpu.roll(mask_whole, rows, 1).reshape(cols, depth)
    masks = []
    for jh in range(per_row):
        right_t = jnp.transpose(right_whole[jh * LANES : (jh + 1) * LANES])
        masks.append(jnp.transpose(mask_whole[jh * LANES : (jh + 1) * LANES])[:1])
        for r in range(rows):
            m = r * per_row + jh
            pair[m] = (base[m] + right_t).astype(BF16).astype(F32)

    for u in range(2):
        local = [
            weights[u, g, pl.ds(pl.multiple_of(x * width, width), width), :] for g in range(4)
        ]
        local = jnp.concatenate(local, axis=0)
        left_parts, right_parts = [], []
        for m in range(blocks):
            block = (norm_rows(pair[m]) * columns[u, 0]).astype(BF16)
            normed[m] = block
            projected = nn(local, block)
            masked = masks[m % per_row] * mask_of[m // per_row]
            value, gate = projected[:width], projected[width : 2 * width]
            left_parts.append((masked * jax.nn.sigmoid(gate) * value).astype(BF16))
            value, gate = projected[2 * width : 3 * width], projected[3 * width :]
            right_parts.append((masked * jax.nn.sigmoid(gate) * value).astype(BF16))
        for side, parts in enumerate((left_parts, right_parts)):
            ordered = nn(perm[...], jnp.concatenate(parts, axis=0)).astype(BF16)
            edges_out[u, side] = ordered.reshape(rings, blocks, LANES)

        for side, buffer in enumerate((left_in.at[u], right_in.at[u])):
            own = lambda peer, side=side: edges_out.at[u, side, peer]
            their = lambda peer, buffer=buffer: buffer.at[h, peer]
            all_send(own, their, edge_send.at[u, side], edge_recv.at[u, side])
            buffer[h, z] = edges_out[u, side, z]
        swaps = []
        for side, buffer in reversed(list(enumerate((left_in.at[u], right_in.at[u])))):
            own = lambda peer, side=side: edges_out.at[u, side, peer]
            their = lambda peer, buffer=buffer: buffer.at[h, peer]
            all_wait(own, their, edge_send.at[u, side], edge_recv.at[u, side], False)
            closing.append(
                functools.partial(
                    all_wait, own, their, edge_send.at[u, side], edge_recv.at[u, side], True
                )
            )
            if side == 1 or u == 1:
                swaps.append(swap(buffer, 1 + 2 * u + side))
        for sent, got in swaps:
            got.wait_recv()
            closing.append(sent.wait_send)

        right_rows_all = right_in[u].reshape(2 * size, LANES)
        if u == 0:
            left_own = left_in[u, h].reshape(size, LANES)
            a = [nn(pick[half], left_own).astype(BF16) for half in range(2)]
            b = [nn(pick_right[half], right_rows_all).astype(BF16) for half in range(2)]
            whole = nt(jnp.concatenate(a, axis=1), jnp.concatenate(b, axis=1))
            even = lax.rem(lax.broadcasted_iota(jnp.int32, (size, LANES), 0), 2) == 0
            product = jnp.where(even, whole[:, :LANES], whole[:, LANES:])
        else:
            spread = []
            for parity in range(2):
                block = left_in[u, parity].reshape(size, LANES)
                halves = [nn(pick[half], block).astype(BF16) for half in range(2)]
                spread.append(jnp.concatenate(halves, axis=1))
            chosen = nt(pick_left[...], jnp.concatenate(spread, axis=0))
            row_half = lax.rem(lax.broadcasted_iota(jnp.int32, chosen.shape, 0), 2)
            column_half = lax.rem(lax.broadcasted_iota(jnp.int32, chosen.shape, 1), 2)
            chosen = jnp.where(row_half == column_half, chosen, 0.0).astype(BF16)
            product = nn(chosen, right_rows_all)
        product_out[u] = product.astype(BF16).reshape(rings, blocks, LANES)

        own = lambda peer: product_out.at[u, peer]
        their = lambda peer: product_in.at[u, x, peer]
        all_send(own, their, back_send.at[u], back_recv.at[u])
        product_in[u, x, z] = product_out[u, z]
        all_wait(own, their, back_send.at[u], back_recv.at[u], False)
        closing.append(functools.partial(all_wait, own, their, back_send.at[u], back_recv.at[u], True))

        def lane_copy(t, source):
            return pltpu.make_async_remote_copy(
                src_ref=product_in.at[u, source],
                dst_ref=product_in.at[u, source],
                send_sem=lane_send.at[u, t],
                recv_sem=lane_recv.at[u, source],
                device_id={"chan": to_x(t)},
                device_id_type=MESH,
            )

        for t in (2, 1, 3) if lanes_x == 4 else range(1, lanes_x):
            lane_copy(t, x).start()
        gating = [
            jax.nn.sigmoid(nn(gate_weights[u], normed[m]) + columns[u, 1]) for m in range(blocks)
        ]
        for t in range(1, lanes_x):
            lane_copy(t, to_x(t)).wait_recv()
            closing.append(lane_copy(t, x).wait_send)
        hidden = [
            nn(perm_back[...], product_in[u, lane].reshape(size, LANES)) for lane in range(lanes_x)
        ]
        for m in range(blocks):
            block = jnp.concatenate([part[m * rings : (m + 1) * rings] for part in hidden], axis=0)
            block = (norm_rows(block) * columns[u, 2]).astype(BF16)
            update = nn(out_weights[u], block)
            value = pair[m] + gating[m] * update
            if u == 0:
                pair[m] = value.astype(BF16).astype(F32)
            else:
                r, jh = m // per_row, m % per_row
                out_ref[r, jh * LANES : (jh + 1) * LANES, :] = jnp.transpose(value).astype(BF16)

    for wait in closing:
        wait()


def body(
    prior_pair,
    single,
    target,
    residue_mask,
    recycle_gain,
    recycle_bias,
    left_single,
    right_single,
    left_target,
    right_target,
    tri_gain,
    tri_proj,
    tri_gate,
    tri_gate_bias,
    tri_out_gain,
    tri_out,
):
    rings = lax.axis_size("dap") // 2
    lanes_x = lax.axis_size("chan")
    rows, cols, depth = prior_pair.shape
    blocks = rows * cols // LANES
    size = rings * blocks
    vmem = pl.BlockSpec(memory_space=pltpu.VMEM)
    smem = pl.BlockSpec(memory_space=pltpu.SMEM)
    dma = pltpu.SemaphoreType.DMA
    return pl.pallas_call(
        functools.partial(kernel, rings, lanes_x),
        out_shape=jax.ShapeDtypeStruct(prior_pair.shape, BF16),
        in_specs=[vmem, vmem, smem, smem] + [vmem] * 12,
        out_specs=vmem,
        scratch_shapes=[
            pltpu.VMEM((2, rings, 2 * rows, LANES), F32),
            pltpu.VMEM((2, 2, rings, blocks, LANES), BF16),
            pltpu.VMEM((2, 2, rings, blocks, LANES), BF16),
            pltpu.VMEM((2, 2, rings, blocks, LANES), BF16),
            pltpu.VMEM((2, rings, blocks, LANES), BF16),
            pltpu.VMEM((2, lanes_x, rings, blocks, LANES), BF16),
            pltpu.VMEM((blocks, depth, LANES), F32),
            pltpu.VMEM((blocks, depth, LANES), F32),
            pltpu.VMEM((blocks, depth, LANES), BF16),
            pltpu.VMEM((2, 4, depth, depth), BF16),
            pltpu.VMEM((2, depth, depth), BF16),
            pltpu.VMEM((2, depth, depth), BF16),
            pltpu.VMEM((2, 3, depth, LANES), F32),
            pltpu.VMEM((size, size), BF16),
            pltpu.VMEM((size, size), BF16),
            pltpu.VMEM((2, size, size), BF16),
            pltpu.VMEM((2, size, 2 * size), BF16),
            pltpu.VMEM((size, cols), BF16),
            dma((rings,)),
            dma((rings,)),
            dma((2, 2, rings)),
            dma((2, 2, rings)),
            dma((2, rings)),
            dma((2, rings)),
            dma((5,)),
            dma((5,)),
            dma((2, lanes_x)),
            dma((2, lanes_x)),
        ],
        compiler_params=pltpu.CompilerParams(collective_id=0, has_side_effects=True),
        name="triangles",
    )(
        prior_pair,
        single,
        target,
        residue_mask,
        recycle_gain[None, :],
        recycle_bias[None, :],
        left_single,
        right_single,
        left_target,
        right_target,
        tri_gain,
        tri_proj.reshape(2, depth, -1),
        tri_gate,
        tri_gate_bias,
        tri_out_gain,
        tri_out,
    )


def solution(mesh):
    rows = P(("crops", "dap"))
    placed = (P(("crops", "dap"), None, None), P(("crops", "dap"), None), rows, rows) + (P(),) * 12
    return jax.shard_map(
        body, mesh=mesh, in_specs=placed, out_specs=P(("crops", "dap"), None, None), check_vma=False
    )
```

time: 409 us -> 159 us (0.39)
  waiting for transfers between devices: 245 us -> 0 us
  Pallas kernels: 0 us -> 155 us
  blocking collectives: 97.4 us -> 0 us
  starting transfers between devices: 22.7 us -> 0 us
  matrix products: 15.1 us -> 0 us
  between operations: 13.7 us -> 0.01 us
  other arithmetic: 8.15 us -> 0 us
    all_gather x2 -> x0, waiting for transfers between devices: 209 us -> none  [the longest x1 121 us: body(): lax.all_gather(outgoing_right_edges, 'dap', axis=1, tiled=True)]
    pallas_call x0 -> x1, Pallas kernels: none -> 155 us  [body(): pl.pallas_call(functools.partial(kernel, rings, lanes_x), out_shape=jax.S...]
    all_gather x1 -> x0, blocking collectives: 97.4 us -> none  [side_by_side(): out = lax.all_gather(both, axis, axis=dim, tiled=True)]
    all_to_all x3 -> x0, waiting for transfers between devices: 36.1 us -> none  [the longest x1 24.9 us: body(): lax.all_to_all(left_edges, 'dap', split_axis=2, concat_axis=1, tiled=True)]
    all_to_all x3 -> x0, starting transfers between devices: 22.7 us -> none  [the longest x1 14.6 us: body(): lax.all_to_all(left_edges, 'dap', split_axis=2, concat_axis=1, tiled=True)]
    dot_general x12 -> x0, matrix products: 15.1 us -> none  [the longest x1 4.55 us: body(): jnp.einsum('cik,cjk->cij', outgoing_left_edges, lax.all_gather(outgoing_r...]
    reduce_sum x9 -> x0, other arithmetic: 5 us -> none  [the longest x4 2.71 us: layer_norm(): center = values - jnp.mean(values, axis=axis, keepdims=True)]
  transfers between devices with their start and end apart: 5 -> 0, of which waited for: 5 -> 0; matrix products, arithmetic and copies ran while one was open for 1% -> 0% of each run, Pallas kernels for 0% -> 0%
where the time goes in v1:
time: 159 us
  Pallas kernels  155 us (97%)
  local copies, waits for them, and re-layouts  3.42 us (2%)
    pallas_call x1, Pallas kernels, body(): pl.pallas_call(functools.partial(kernel, rings, lanes_x), out_shape=jax.S...  155 us

profile of v1, /device:TPU:33, one launch (start us, length us, event | category | flops | bytes accessed | tf_op | source)
XLA Modules:
  0.0 158.8 jit_solution(9997471356026191760)
XLA Ops:
  0.0 1.8 %reshape.3.tri_proj_ref = bf16[2,128,512]{2,1,0:T(8,128)(2,1)} reshape(bf16[2,128,4,128]{3,2,1,0:T(4,128)(2,1)} %param.27) | data formatting | bytes 524288 | tf_op jit(solution)/shard_map/reshape | solution.py:428
  1.8 155.4 %triangles.1 = bf16[4,256,128]{2,1,0:T(8,128)(2,1)} custom-call(bf16[4,256,128]{2,1,0:T(8,128)(2,1)} %prior_ref.1, bf16[4,384]{1,0:T(4,128)(2,1)} %single_ref.1, s32[4]{0:T(128)} %target_ref.1, s32[4]{0:T(128)} %mask_ref.1, f32[1,128]{1,0:T(1,128)} %bitcast.2, f32[1,128]{1,0:T(1,128)} %bitcast.3, bf16[384,128]{1,0:T(8,128)(2,1)} %left_single_ref.1, ...), custom_call_target="tpu_custom_call" | custom-call | tf_op jit(solution)/shard_map/triangles/pallas_call | solution.py:379
  157.2 1.7 %copy.18 = bf16[4,256,128]{2,1,0:T(8,128)(2,1)} copy(bf16[4,256,128]{2,1,0:T(8,128)(2,1)} %triangles.1) | data formatting | bytes 524288

commit v2 on v1

v2 whole, which is shorter than its diff:
```python
import functools

import jax
import jax.numpy as jnp
from jax import lax
from jax.experimental import pallas as pl
from jax.experimental.pallas import tpu as pltpu
from jax.sharding import PartitionSpec as P

F32 = jnp.float32
BF16 = jnp.bfloat16
MESH = pl.DeviceIdType.MESH
EPS = 1e-05
LANES = 128
GROUP = 8


def selection(shape, column_of_row):
    rows = lax.broadcasted_iota(jnp.int32, shape, 0)
    columns = lax.broadcasted_iota(jnp.int32, shape, 1)
    return jnp.where(columns == column_of_row(rows), 1.0, 0.0).astype(BF16)


def nn(a, b):
    return lax.dot_general(a, b, (((1,), (0,)), ((), ())), preferred_element_type=F32)


def nt(a, b):
    return lax.dot_general(a, b, (((1,), (1,)), ((), ())), preferred_element_type=F32)


def norm_rows(values):
    scale = 1.0 / values.shape[0]
    center = values - jnp.sum(values, axis=0, keepdims=True) * scale
    spread = jnp.sum(center * center, axis=0, keepdims=True) * scale
    return center * lax.rsqrt(spread + EPS)


class Phases:
    def __init__(self):
        self.scope = None

    def __call__(self, name):
        if self.scope is not None:
            self.scope.__exit__(None, None, None)
        self.scope = jax.named_scope(name) if name else None
        if self.scope is not None:
            self.scope.__enter__()


def column(row_vector):
    return jnp.transpose(jnp.broadcast_to(row_vector, (LANES, LANES)))


def kernel(
    rings,
    lanes_x,
    prior_hbm,
    single_hbm,
    target_hbm,
    mask_hbm,
    recycle_gain_hbm,
    recycle_bias_hbm,
    left_single_hbm,
    right_single_hbm,
    left_target_hbm,
    right_target_hbm,
    tri_gain_hbm,
    tri_proj_hbm,
    tri_gate_hbm,
    tri_gate_bias_hbm,
    tri_out_gain_hbm,
    tri_out_hbm,
    out_ref,
    prior_ref,
    single_ref,
    target_ref,
    mask_ref,
    recycle_gain_ref,
    recycle_bias_ref,
    left_single_ref,
    right_single_ref,
    left_target_ref,
    right_target_ref,
    tri_gain_ref,
    tri_proj_ref,
    tri_gate_ref,
    tri_gate_bias_ref,
    tri_out_gain_ref,
    tri_out_ref,
    terms,
    edges_out,
    edges_in,
    product_out,
    product_in,
    base,
    pair,
    normed,
    weights,
    gate_weights,
    out_weights,
    columns,
    perm,
    perm_back,
    pick,
    pick_right,
    pick_left,
    load_sem,
    terms_sem,
    edge_sem,
    back_send,
    back_recv,
    twin_send,
    twin_recv,
    lane_sem,
):
    rows, cols, depth = prior_ref.shape
    blocks = rows * cols // LANES
    per_row = cols // LANES
    width = depth // lanes_x
    size = rings * blocks
    dap = lax.axis_index("dap")
    x = lax.axis_index("chan")
    z = dap // 2
    h = lax.rem(dap, 2)
    twin = {"dap": dap + 1 - 2 * h}
    phase = Phases()

    def offset(p):
        up = (p + 1) // 2
        return rings + up * (2 * lax.rem(p, 2) - 1)

    def to_z(peer):
        return {"dap": 2 * peer + h}

    def to_x(t):
        return lax.rem(x + t, lanes_x)

    phase("greet")
    barrier = pltpu.get_barrier_semaphore()

    def greet(t, carry):
        peer = lax.rem(z + offset(rings - 1 - t), rings)
        pl.semaphore_signal(barrier, inc=1, device_id=to_z(peer), device_id_type=MESH)
        return carry

    lax.fori_loop(0, rings - 1, greet, 0)
    pl.semaphore_signal(barrier, inc=1, device_id=twin, device_id_type=MESH)
    for t in range(1, lanes_x):
        pl.semaphore_signal(barrier, inc=1, device_id={"chan": to_x(t)}, device_id_type=MESH)

    loads = {}
    sources = (
        (single_hbm, single_ref),
        (right_single_hbm, right_single_ref),
        (target_hbm, target_ref),
        (mask_hbm, mask_ref),
        (right_target_hbm, right_target_ref),
        (left_single_hbm, left_single_ref),
        (left_target_hbm, left_target_ref),
        (recycle_gain_hbm, recycle_gain_ref),
        (recycle_bias_hbm, recycle_bias_ref),
        (prior_hbm, prior_ref),
        (tri_proj_hbm, tri_proj_ref),
        (tri_gain_hbm, tri_gain_ref),
        (tri_gate_hbm, tri_gate_ref),
        (tri_gate_bias_hbm, tri_gate_bias_ref),
        (tri_out_gain_hbm, tri_out_gain_ref),
        (tri_out_hbm, tri_out_ref),
    )
    loads = [
        pltpu.make_async_copy(source, held, load_sem.at[n])
        for n, (source, held) in enumerate(sources)
    ]
    for load in loads:
        load.start()

    phase("terms")
    for load in loads[:5]:
        load.wait()
    single = single_ref[...]
    mask_of = [mask_ref[r].astype(F32) for r in range(rows)]

    def row_terms(weight_ref, table_ref):
        linear = nn(single, weight_ref[...])
        table = table_ref[...].astype(F32)
        classes = lax.broadcasted_iota(jnp.int32, table.shape, 0)
        picked = [
            jnp.sum(jnp.where(classes == target_ref[r], table, 0.0), axis=0, keepdims=True)
            for r in range(rows)
        ]
        return [linear[r : r + 1] + picked[r] for r in range(rows)]

    right_rows = row_terms(right_single_ref, right_target_ref)
    mask_rows = [jnp.full((1, depth), mask_of[r], F32) for r in range(rows)]
    tile = jnp.concatenate(right_rows + mask_rows, axis=0)
    terms[h, z] = jnp.where(h == 0, tile, pltpu.roll(tile, rows, 0))

    phase("barrier")
    pl.semaphore_wait(barrier, rings - 1 + 1 + lanes_x - 1)

    def remote(source, target, send, recv, device):
        return pltpu.make_async_remote_copy(
            src_ref=source,
            dst_ref=target,
            send_sem=send,
            recv_sem=recv,
            device_id=device,
            device_id_type=MESH,
        )

    closing = []

    phase("tsend")

    def send_terms(t, carry):
        peer = lax.rem(z + offset(rings - 1 - t), rings)
        remote(terms.at[h, z], terms.at[h, z], terms_sem.at[0], terms_sem.at[1], to_z(peer)).start()
        return carry

    lax.fori_loop(0, rings - 1, send_terms, 0)
    many = terms.at[h, pl.ds(0, rings - 1)]
    terms_all = remote(many, many, terms_sem.at[0], terms_sem.at[1], twin)
    closing.append(terms_all.wait_send)

    phase("local")
    for load in loads[5:]:
        load.wait()
    left_rows = row_terms(left_single_ref, left_target_ref)
    gain = recycle_gain_ref[...]
    bias = recycle_bias_ref[...]
    for r in range(rows):
        for jh in range(per_row):
            block = prior_ref[r, jh * LANES : (jh + 1) * LANES, :].astype(F32)
            center = block - jnp.mean(block, axis=1, keepdims=True)
            spread = jnp.mean(center * center, axis=1, keepdims=True)
            value = center * lax.rsqrt(spread + EPS) * gain + bias + left_rows[r]
            base[r * per_row + jh] = jnp.transpose(value)
    for u in range(2):
        whole = tri_proj_ref[u].astype(F32)
        for g in range(4):
            weights[u, g] = jnp.transpose(whole[:, g, :]).astype(BF16)
        gate_weights[u] = jnp.transpose(tri_gate_ref[u].astype(F32)).astype(BF16)
        out_weights[u] = jnp.transpose(tri_out_ref[u].astype(F32)).astype(BF16)
        columns[u, 0] = column(tri_gain_ref[u : u + 1, :])
        columns[u, 1] = column(tri_gate_bias_ref[u : u + 1, :])
        columns[u, 2] = column(tri_out_gain_ref[u : u + 1, :])

    def place(channel):
        delta = lax.rem(channel - z + rings, rings)
        after = jnp.where(delta <= rings // 2, 2 * delta - 1, 2 * (rings - delta))
        return jnp.where(delta == 0, 0, after)

    perm[...] = selection((size, size), lambda q: lax.rem(q, blocks) * rings + q // blocks)
    perm_back[...] = selection(
        (size, size), lambda q: place(lax.rem(q, rings)) * blocks + q // rings
    )
    for half in range(2):
        pick[half] = selection((size, size), lambda q: q - lax.rem(q, 2) + half)
        pick_right[half] = selection(
            (size, 2 * size),
            lambda j: lax.rem(j // rows, 2) * size
            + (j // (2 * rows)) * blocks
            + 2 * lax.rem(j, rows)
            + half,
        )
    pick_left[...] = selection(
        (size, cols), lambda q: (q // blocks) * 2 * rows + rows * h + lax.rem(q, blocks) // 2
    )

    phase("twait")
    terms_all.wait_recv()
    phase("ttwin")

    def swap(view, k):
        def copy(parity):
            return remote(view(parity), view(parity), twin_send.at[k], twin_recv.at[k], twin)

        copy(h).start()
        closing.append(copy(h).wait_send)
        copy(1 - h).wait_recv()

    swap(lambda parity: terms.at[parity], 0)

    phase("pair")
    first, second = terms[0], terms[1]
    upper = lax.broadcasted_iota(jnp.int32, first.shape, 1) < rows
    right_whole = jnp.where(upper, first, second).reshape(cols, depth)
    mask_whole = jnp.where(upper, second, first)
    mask_whole = pltpu.roll(mask_whole, rows, 1).reshape(cols, depth)
    masks = []
    for jh in range(per_row):
        right_t = jnp.transpose(right_whole[jh * LANES : (jh + 1) * LANES])
        masks.append(jnp.transpose(mask_whole[jh * LANES : (jh + 1) * LANES])[:1])
        for r in range(rows):
            m = r * per_row + jh
            pair[m] = (base[m] + right_t).astype(BF16).astype(F32)

    for u in range(2):
        phase("edges")
        local = [
            weights[u, g, pl.ds(pl.multiple_of(x * width, width), width), :] for g in range(4)
        ]
        local = jnp.concatenate(local, axis=0)
        left_parts, right_parts = [], []
        for m in range(blocks):
            block = (norm_rows(pair[m]) * columns[u, 0]).astype(BF16)
            normed[m] = block
            projected = nn(local, block)
            masked = masks[m % per_row] * mask_of[m // per_row]
            value, gate = projected[:width], projected[width : 2 * width]
            left_parts.append((masked * jax.nn.sigmoid(gate) * value).astype(BF16))
            value, gate = projected[2 * width : 3 * width], projected[3 * width :]
            right_parts.append((masked * jax.nn.sigmoid(gate) * value).astype(BF16))
        for side, parts in enumerate((left_parts, right_parts)):
            ordered = nn(perm[...], jnp.concatenate(parts, axis=0)).astype(BF16)
            edges_out[u, :, side] = ordered.reshape(rings, blocks, LANES)

        phase("esend")

        def send_edges(t, carry, u=u):
            peer = lax.rem(z + offset(rings - 1 - t), rings)
            remote(
                edges_out.at[u, peer],
                edges_in.at[u, h, z],
                edge_sem.at[u, 0],
                edge_sem.at[u, 1],
                to_z(peer),
            ).start()
            return carry

        lax.fori_loop(0, rings - 1, send_edges, 0)
        edges_in[u, h, z] = edges_out[u, z]
        gating = [
            jax.nn.sigmoid(nn(gate_weights[u], normed[m]) + columns[u, 1]) for m in range(blocks)
        ]
        many = edges_in.at[u, h, pl.ds(0, rings - 1)]
        edges_all = remote(many, many, edge_sem.at[u, 0], edge_sem.at[u, 1], twin)
        closing.append(edges_all.wait_send)
        phase("ewait")
        edges_all.wait_recv()
        phase("etwin")
        if u == 0:
            swap(lambda parity: edges_in.at[0, parity, :, 1], 1)
        else:
            swap(lambda parity: edges_in.at[1, parity], 2)

        phase("product")
        right_rows_all = edges_in[u, :, :, 1].reshape(2 * size, LANES)
        if u == 0:
            left_own = edges_in[u, h, :, 0].reshape(size, LANES)
            a = [nn(pick[half], left_own).astype(BF16) for half in range(2)]
            b = [nn(pick_right[half], right_rows_all).astype(BF16) for half in range(2)]
            whole = nt(jnp.concatenate(a, axis=1), jnp.concatenate(b, axis=1))
            even = lax.rem(lax.broadcasted_iota(jnp.int32, (size, LANES), 0), 2) == 0
            product = jnp.where(even, whole[:, :LANES], whole[:, LANES:])
        else:
            spread = []
            for parity in range(2):
                block = edges_in[u, parity, :, 0].reshape(size, LANES)
                halves = [nn(pick[half], block).astype(BF16) for half in range(2)]
                spread.append(jnp.concatenate(halves, axis=1))
            chosen = nt(pick_left[...], jnp.concatenate(spread, axis=0))
            row_half = lax.rem(lax.broadcasted_iota(jnp.int32, chosen.shape, 0), 2)
            column_half = lax.rem(lax.broadcasted_iota(jnp.int32, chosen.shape, 1), 2)
            chosen = jnp.where(row_half == column_half, chosen, 0.0).astype(BF16)
            product = nn(chosen, right_rows_all)
        product_out[u] = product.astype(BF16).reshape(rings, blocks, LANES)

        phase("bsend")

        def send_back(t, carry, u=u):
            p = rings - 1 - t
            peer = lax.rem(z + 2 * rings - offset(p), rings)
            remote(
                product_out.at[u, peer],
                product_in.at[u, x, p],
                back_send.at[u],
                back_recv.at[u, (p - 1) // GROUP],
                to_z(peer),
            ).start()
            return carry

        lax.fori_loop(0, rings - 1, send_back, 0)
        product_in[u, x, 0] = product_out[u, z]
        many = product_out.at[u, pl.ds(0, rings - 1)]
        closing.append(remote(many, many, back_send.at[u], back_recv.at[u, 0], twin).wait_send)
        phase("bwait")
        for g, start in enumerate(range(1, rings, GROUP)):
            arrived = product_in.at[u, x, pl.ds(start, min(GROUP, rings - start))]
            remote(arrived, arrived, back_send.at[u], back_recv.at[u, g], twin).wait_recv()
            begin = start if g else 0
            part = product_in.at[u, x, pl.ds(begin, min(start + GROUP, rings) - begin)]
            for t in (2, 1, 3) if lanes_x == 4 else range(1, lanes_x):
                remote(part, part, lane_sem.at[u, 0], lane_sem.at[u, 1], {"chan": to_x(t)}).start()
        phase("lwait")
        many = product_in.at[u, pl.ds(0, lanes_x - 1)]
        lanes_all = remote(many, many, lane_sem.at[u, 0], lane_sem.at[u, 1], twin)
        lanes_all.wait_recv()
        closing.append(lanes_all.wait_send)

        phase("hidden")
        hidden = [
            nn(perm_back[...], product_in[u, lane].reshape(size, LANES)) for lane in range(lanes_x)
        ]
        for m in range(blocks):
            block = jnp.concatenate([part[m * rings : (m + 1) * rings] for part in hidden], axis=0)
            block = (norm_rows(block) * columns[u, 2]).astype(BF16)
            update = nn(out_weights[u], block)
            value = pair[m] + gating[m] * update
            if u == 0:
                pair[m] = value.astype(BF16).astype(F32)
            else:
                r, jh = m // per_row, m % per_row
                out_ref[r, jh * LANES : (jh + 1) * LANES, :] = jnp.transpose(value).astype(BF16)

    phase("close")
    for wait in closing:
        wait()
    phase(None)


def body(
    prior_pair,
    single,
    target,
    residue_mask,
    recycle_gain,
    recycle_bias,
    left_single,
    right_single,
    left_target,
    right_target,
    tri_gain,
    tri_proj,
    tri_gate,
    tri_gate_bias,
    tri_out_gain,
    tri_out,
):
    rings = lax.axis_size("dap") // 2
    lanes_x = lax.axis_size("chan")
    rows, cols, depth = prior_pair.shape
    blocks = rows * cols // LANES
    size = rings * blocks
    groups = -(-(rings - 1) // GROUP)
    vmem = pl.BlockSpec(memory_space=pltpu.VMEM)
    hbm = pl.BlockSpec(memory_space=pltpu.HBM)
    dma = pltpu.SemaphoreType.DMA
    operands = (
        prior_pair,
        single,
        target,
        residue_mask,
        recycle_gain[None, :],
        recycle_bias[None, :],
        left_single,
        right_single,
        left_target,
        right_target,
        tri_gain,
        tri_proj,
        tri_gate,
        tri_gate_bias,
        tri_out_gain,
        tri_out,
    )
    held = [
        pltpu.SMEM(a.shape, a.dtype) if a.dtype == jnp.int32 else pltpu.VMEM(a.shape, a.dtype)
        for a in operands
    ]
    return pl.pallas_call(
        functools.partial(kernel, rings, lanes_x),
        out_shape=jax.ShapeDtypeStruct(prior_pair.shape, BF16),
        in_specs=[hbm] * len(operands),
        out_specs=vmem,
        scratch_shapes=held
        + [
            pltpu.VMEM((2, rings, 2 * rows, LANES), F32),
            pltpu.VMEM((2, rings, 2, blocks, LANES), BF16),
            pltpu.VMEM((2, 2, rings, 2, blocks, LANES), BF16),
            pltpu.VMEM((2, rings, blocks, LANES), BF16),
            pltpu.VMEM((2, lanes_x, rings, blocks, LANES), BF16),
            pltpu.VMEM((blocks, depth, LANES), F32),
            pltpu.VMEM((blocks, depth, LANES), F32),
            pltpu.VMEM((blocks, depth, LANES), BF16),
            pltpu.VMEM((2, 4, depth, depth), BF16),
            pltpu.VMEM((2, depth, depth), BF16),
            pltpu.VMEM((2, depth, depth), BF16),
            pltpu.VMEM((2, 3, depth, LANES), F32),
            pltpu.VMEM((size, size), BF16),
            pltpu.VMEM((size, size), BF16),
            pltpu.VMEM((2, size, size), BF16),
            pltpu.VMEM((2, size, 2 * size), BF16),
            pltpu.VMEM((size, cols), BF16),
            dma((len(operands),)),
            dma((2,)),
            dma((2, 2)),
            dma((2,)),
            dma((2, groups)),
            dma((3,)),
            dma((3,)),
            dma((2, 2)),
        ],
        compiler_params=pltpu.CompilerParams(collective_id=0, has_side_effects=True),
        name="triangles",
    )(*operands)


def solution(mesh):
    rows = P(("crops", "dap"))
    placed = (P(("crops", "dap"), None, None), P(("crops", "dap"), None), rows, rows) + (P(),) * 12
    return jax.shard_map(
        body, mesh=mesh, in_specs=placed, out_specs=P(("crops", "dap"), None, None), check_vma=False
    )
```

time: 159 us -> 140 us (0.88)
  Pallas kernels: 155 us -> 138 us
  local copies, waits for them, and re-layouts: 3.42 us -> 1.67 us
    pallas_call x1, Pallas kernels: 155 us -> 138 us  [body(): pl.pallas_call(functools.partial(kernel, rings, lanes_x), out_shape=jax.S...]
    reshape x1 -> x0, local copies, waits for them, and re-layouts: 1.75 us -> none  [body(): tri_proj.reshape(2, depth, -1)]
where the time goes in v2:
time: 140 us
  Pallas kernels  138 us (99%)
  local copies, waits for them, and re-layouts  1.67 us (1%)
    pallas_call x1, Pallas kernels, body(): pl.pallas_call(functools.partial(kernel, rings, lanes_x), out_shape=jax.S...  138 us

profile of v2, /device:TPU:33, one launch (start us, length us, event | category | flops | bytes accessed | tf_op | source)
XLA Modules:
  0.0 139.9 jit_solution(2941344613972939667)
XLA Ops:
  0.0 138.2 %triangles.1 = bf16[4,256,128]{2,1,0:T(8,128)(2,1)} custom-call(bf16[4,256,128]{2,1,0:T(8,128)(2,1)} %prior_hbm.1, bf16[4,384]{1,0:T(4,128)(2,1)} %single_hbm.1, s32[4]{0:T(128)} %target_hbm.1, s32[4]{0:T(128)} %mask_hbm.1, f32[1,128]{1,0:T(1,128)} %bitcast.2, f32[1,128]{1,0:T(1,128)} %bitcast.3, bf16[384,128]{1,0:T(8,128)(2,1)} %left_single_hbm.1, ...), custom_call_target="tpu_custom_call" | custom-call | tf_op jit(solution)/shard_map/triangles/pallas_call | solution.py:472
  138.3 1.7 %copy.18 = bf16[4,256,128]{2,1,0:T(8,128)(2,1)} copy(bf16[4,256,128]{2,1,0:T(8,128)(2,1)} %triangles.1) | data formatting | bytes 524288

commit v3 on v2

--- a/solution.py
+++ b/solution.py
@@ -13,6 +13,7 @@
 EPS = 1e-05
 LANES = 128
 GROUP = 8
+STRIDE = 4
 
 
 def selection(shape, column_of_row):
@@ -106,7 +107,8 @@
     pick_right,
     pick_left,
     load_sem,
-    terms_sem,
+    terms_send,
+    terms_recv,
     edge_sem,
     back_send,
     back_recv,
@@ -139,17 +141,21 @@
     phase("greet")
     barrier = pltpu.get_barrier_semaphore()
 
-    def greet(t, carry):
-        peer = lax.rem(z + offset(rings - 1 - t), rings)
-        pl.semaphore_signal(barrier, inc=1, device_id=to_z(peer), device_id_type=MESH)
-        return carry
-
-    lax.fori_loop(0, rings - 1, greet, 0)
+    q = lax.rem(z + rings - 1, rings)
+    last = rings - 1
+
+    def at(order):
+        return to_z(lax.rem(order + 1, rings))
+
+    def greet(order):
+        pl.semaphore_signal(barrier, inc=1, device_id=at(order), device_id_type=MESH)
+
+    for back in range(1, STRIDE + 1):
+        pl.when(q >= back)(functools.partial(greet, q - back))
     pl.semaphore_signal(barrier, inc=1, device_id=twin, device_id_type=MESH)
     for t in range(1, lanes_x):
         pl.semaphore_signal(barrier, inc=1, device_id={"chan": to_x(t)}, device_id_type=MESH)
 
-    loads = {}
     sources = (
         (single_hbm, single_ref),
         (right_single_hbm, right_single_ref),
@@ -175,6 +181,12 @@
     for load in loads:
         load.start()
 
+    def greet_later(order, carry):
+        greet(order)
+        return carry
+
+    lax.fori_loop(q + 1, rings, greet_later, 0)
+
     phase("terms")
     for load in loads[:5]:
         load.wait()
@@ -197,7 +209,7 @@
     terms[h, z] = jnp.where(h == 0, tile, pltpu.roll(tile, rows, 0))
 
     phase("barrier")
-    pl.semaphore_wait(barrier, rings - 1 + 1 + lanes_x - 1)
+    pl.semaphore_wait(barrier, q + jnp.minimum(STRIDE, last - q) + 1 + lanes_x - 1)
 
     def remote(source, target, send, recv, device):
         return pltpu.make_async_remote_copy(
@@ -213,63 +225,124 @@
 
     phase("tsend")
 
-    def send_terms(t, carry):
-        peer = lax.rem(z + offset(rings - 1 - t), rings)
-        remote(terms.at[h, z], terms.at[h, z], terms_sem.at[0], terms_sem.at[1], to_z(peer)).start()
+    def give(source, order):
+        tile = terms.at[h, source]
+        remote(tile, tile, terms_send.at[0], terms_recv.at[source], at(order)).start()
+
+    def carried(source):
+        return lax.rem(source, lanes_x) == x
+
+    for ahead in range(1, STRIDE + 1):
+        pl.when(carried(z) & (q + ahead <= last))(functools.partial(give, z, q + ahead))
+
+    def give_earlier(t, carry):
+        order = lax.rem(q + offset(rings - 1 - t), rings)
+        pl.when(order < q)(functools.partial(give, z, order))
         return carry
 
-    lax.fori_loop(0, rings - 1, send_terms, 0)
-    many = terms.at[h, pl.ds(0, rings - 1)]
-    terms_all = remote(many, many, terms_sem.at[0], terms_sem.at[1], twin)
-    closing.append(terms_all.wait_send)
-
-    phase("local")
-    for load in loads[5:]:
-        load.wait()
-    left_rows = row_terms(left_single_ref, left_target_ref)
-    gain = recycle_gain_ref[...]
-    bias = recycle_bias_ref[...]
-    for r in range(rows):
-        for jh in range(per_row):
-            block = prior_ref[r, jh * LANES : (jh + 1) * LANES, :].astype(F32)
-            center = block - jnp.mean(block, axis=1, keepdims=True)
-            spread = jnp.mean(center * center, axis=1, keepdims=True)
-            value = center * lax.rsqrt(spread + EPS) * gain + bias + left_rows[r]
-            base[r * per_row + jh] = jnp.transpose(value)
-    for u in range(2):
-        whole = tri_proj_ref[u].astype(F32)
-        for g in range(4):
-            weights[u, g] = jnp.transpose(whole[:, g, :]).astype(BF16)
-        gate_weights[u] = jnp.transpose(tri_gate_ref[u].astype(F32)).astype(BF16)
-        out_weights[u] = jnp.transpose(tri_out_ref[u].astype(F32)).astype(BF16)
-        columns[u, 0] = column(tri_gain_ref[u : u + 1, :])
-        columns[u, 1] = column(tri_gate_bias_ref[u : u + 1, :])
-        columns[u, 2] = column(tri_out_gain_ref[u : u + 1, :])
-
-    def place(channel):
-        delta = lax.rem(channel - z + rings, rings)
-        after = jnp.where(delta <= rings // 2, 2 * delta - 1, 2 * (rings - delta))
-        return jnp.where(delta == 0, 0, after)
-
-    perm[...] = selection((size, size), lambda q: lax.rem(q, blocks) * rings + q // blocks)
-    perm_back[...] = selection(
-        (size, size), lambda q: place(lax.rem(q, rings)) * blocks + q // rings
-    )
-    for half in range(2):
-        pick[half] = selection((size, size), lambda q: q - lax.rem(q, 2) + half)
-        pick_right[half] = selection(
-            (size, 2 * size),
-            lambda j: lax.rem(j // rows, 2) * size
-            + (j // (2 * rows)) * blocks
-            + 2 * lax.rem(j, rows)
-            + half,
+    lax.fori_loop(0, rings - 1, give_earlier, 0)
+
+    def await_terms(source):
+        tile = terms.at[h, source]
+        remote(tile, tile, terms_send.at[0], terms_recv.at[source], twin).wait_recv()
+
+    early = q + STRIDE <= last
+
+    def lower(order):
+        return lax.rem(order + 1, rings)
+
+    def hand_over(source):
+        tile = terms.at[h, source]
+        for lane in range(1, lanes_x):
+            to = {"chan": to_x(lane)}
+            remote(tile, tile, terms_send.at[0], terms_recv.at[source], to).start()
+
+    def relay(order, carry):
+        source = lower(order)
+
+        @pl.when(carried(source))
+        def _():
+            await_terms(source)
+            pl.when(early)(functools.partial(give, source, q + STRIDE))
+            pl.when(jnp.logical_not(early))(functools.partial(hand_over, source))
+
+        return carry
+
+    def hand_over_all(order, carry):
+        source = lower(order)
+        pl.when(carried(source))(functools.partial(hand_over, source))
+        return carry
+
+    def relay_all():
+        lax.fori_loop(0, q, relay, 0)
+        lax.fori_loop(0, jnp.where(early, q, 0), hand_over_all, 0)
+
+    def collect(order, carry):
+        source = lower(order)
+        pl.when(jnp.logical_not(carried(source)))(functools.partial(await_terms, source))
+        return carry
+
+    def prepare():
+        for load in loads[5:]:
+            load.wait()
+        left_rows = row_terms(left_single_ref, left_target_ref)
+        gain = recycle_gain_ref[...]
+        bias = recycle_bias_ref[...]
+        for r in range(rows):
+            for jh in range(per_row):
+                block = prior_ref[r, jh * LANES : (jh + 1) * LANES, :].astype(F32)
+                center = block - jnp.mean(block, axis=1, keepdims=True)
+                spread = jnp.mean(center * center, axis=1, keepdims=True)
+                value = center * lax.rsqrt(spread + EPS) * gain + bias + left_rows[r]
+                base[r * per_row + jh] = jnp.transpose(value)
+        for u in range(2):
+            whole = tri_proj_ref[u].astype(F32)
+            for g in range(4):
+                weights[u, g] = jnp.transpose(whole[:, g, :]).astype(BF16)
+            gate_weights[u] = jnp.transpose(tri_gate_ref[u].astype(F32)).astype(BF16)
+            out_weights[u] = jnp.transpose(tri_out_ref[u].astype(F32)).astype(BF16)
+            columns[u, 0] = column(tri_gain_ref[u : u + 1, :])
+            columns[u, 1] = column(tri_gate_bias_ref[u : u + 1, :])
+            columns[u, 2] = column(tri_out_gain_ref[u : u + 1, :])
+
+        def place(channel):
+            delta = lax.rem(channel - z + rings, rings)
+            after = jnp.where(delta <= rings // 2, 2 * delta - 1, 2 * (rings - delta))
+            return jnp.where(delta == 0, 0, after)
+
+        perm[...] = selection((size, size), lambda q: lax.rem(q, blocks) * rings + q // blocks)
+        perm_back[...] = selection(
+            (size, size), lambda q: place(lax.rem(q, rings)) * blocks + q // rings
         )
-    pick_left[...] = selection(
-        (size, cols), lambda q: (q // blocks) * 2 * rows + rows * h + lax.rem(q, blocks) // 2
-    )
+        for half in range(2):
+            pick[half] = selection((size, size), lambda q: q - lax.rem(q, 2) + half)
+            pick_right[half] = selection(
+                (size, 2 * size),
+                lambda j: lax.rem(j // rows, 2) * size
+                + (j // (2 * rows)) * blocks
+                + 2 * lax.rem(j, rows)
+                + half,
+            )
+        pick_left[...] = selection(
+            (size, cols), lambda q: (q // blocks) * 2 * rows + rows * h + lax.rem(q, blocks) // 2
+        )
+
+    phase("relay")
+
+    def turn(step, carry):
+        pl.when((step == 0) == early)(relay_all)
+        pl.when((step == 1) == early)(prepare)
+        return carry
+
+    lax.fori_loop(0, 2, turn, 0)
 
     phase("twait")
-    terms_all.wait_recv()
+    def later(order, carry):
+        await_terms(lax.rem(order + 1, rings))
+        return carry
+
+    lax.fori_loop(0, q, collect, 0)
+    lax.fori_loop(q + 1, rings, later, 0)
     phase("ttwin")
 
     def swap(view, k):
@@ -337,6 +410,18 @@
         many = edges_in.at[u, h, pl.ds(0, rings - 1)]
         edges_all = remote(many, many, edge_sem.at[u, 0], edge_sem.at[u, 1], twin)
         closing.append(edges_all.wait_send)
+        if u == 0:
+            relayed = (q - x + lanes_x) // lanes_x - jnp.where(x == 0, 1, 0)
+            copies = lanes_x - 1 + jnp.where(q + STRIDE <= last, 1, 0)
+            ahead = jnp.where(carried(z), jnp.minimum(STRIDE, last - q), 0)
+            given = ahead + q + relayed * copies
+
+            def gone(t, carry):
+                tile = terms.at[h, z]
+                remote(tile, tile, terms_send.at[0], terms_recv.at[z], twin).wait_send()
+                return carry
+
+            lax.fori_loop(0, given, gone, 0)
         phase("ewait")
         edges_all.wait_recv()
         phase("etwin")
@@ -494,7 +579,8 @@
             pltpu.VMEM((2, size, 2 * size), BF16),
             pltpu.VMEM((size, cols), BF16),
             dma((len(operands),)),
-            dma((2,)),
+            dma((1,)),
+            dma((rings,)),
             dma((2, 2)),
             dma((2,)),
             dma((2, groups)),

time: 140 us -> 134 us (0.957)
  Pallas kernels: 138 us -> 132 us
    pallas_call x1, Pallas kernels: 138 us -> 132 us  [body(): pl.pallas_call(functools.partial(kernel, rings, lanes_x), out_shape=jax.S...]
where the time goes in v3:
time: 134 us
  Pallas kernels  132 us (99%)
  local copies, waits for them, and re-layouts  1.67 us (1%)
    pallas_call x1, Pallas kernels, body(): pl.pallas_call(functools.partial(kernel, rings, lanes_x), out_shape=jax.S...  132 us

profile of v3, /device:TPU:33, one launch (start us, length us, event | category | flops | bytes accessed | tf_op | source)
XLA Modules:
  0.0 133.9 jit_solution(14235071343012929909)
XLA Ops:
  0.0 132.2 %triangles.1 = bf16[4,256,128]{2,1,0:T(8,128)(2,1)} custom-call(bf16[4,256,128]{2,1,0:T(8,128)(2,1)} %prior_hbm.1, bf16[4,384]{1,0:T(4,128)(2,1)} %single_hbm.1, s32[4]{0:T(128)} %target_hbm.1, s32[4]{0:T(128)} %mask_hbm.1, f32[1,128]{1,0:T(1,128)} %bitcast.2, f32[1,128]{1,0:T(1,128)} %bitcast.3, bf16[384,128]{1,0:T(8,128)(2,1)} %left_single_hbm.1, ...), custom_call_target="tpu_custom_call" | custom-call | tf_op jit(solution)/shard_map/triangles/pallas_call | solution.py:557
  132.2 1.7 %copy.18 = bf16[4,256,128]{2,1,0:T(8,128)(2,1)} copy(bf16[4,256,128]{2,1,0:T(8,128)(2,1)} %triangles.1) | data formatting | bytes 524288

commit v4 on v3

--- a/solution.py
+++ b/solution.py
@@ -14,6 +14,8 @@
 LANES = 128
 GROUP = 8
 STRIDE = 4
+TAIL = 29
+EARLY = 1
 
 
 def selection(shape, column_of_row):
@@ -222,6 +224,11 @@
         )
 
     closing = []
+    starts = [*range(1, TAIL, GROUP), TAIL]
+    spans = list(zip(starts, starts[1:] + [rings]))
+
+    def group_of(p):
+        return (p - 1) // GROUP + jnp.where(p >= TAIL, 1, 0)
 
     phase("tsend")
 
@@ -457,32 +464,70 @@
         def send_back(t, carry, u=u):
             p = rings - 1 - t
             peer = lax.rem(z + 2 * rings - offset(p), rings)
-            remote(
-                product_out.at[u, peer],
-                product_in.at[u, x, p],
-                back_send.at[u],
-                back_recv.at[u, (p - 1) // GROUP],
-                to_z(peer),
-            ).start()
+
+            def send(lane):
+                remote(
+                    product_out.at[u, peer],
+                    product_in.at[u, x, p],
+                    back_send.at[u],
+                    lane_sem.at[u, 1] if lane else back_recv.at[u, group_of(p)],
+                    {"dap": 2 * peer + h, "chan": to_x(lane)} if lane else to_z(peer),
+                ).start()
+
+            send(0)
+            if u:
+
+                @pl.when(peer < EARLY)
+                def _():
+                    for lane in range(1, lanes_x):
+                        send(lane)
+
             return carry
 
         lax.fori_loop(0, rings - 1, send_back, 0)
         product_in[u, x, 0] = product_out[u, z]
-        many = product_out.at[u, pl.ds(0, rings - 1)]
-        closing.append(remote(many, many, back_send.at[u], back_recv.at[u, 0], twin).wait_send)
         phase("bwait")
-        for g, start in enumerate(range(1, rings, GROUP)):
-            arrived = product_in.at[u, x, pl.ds(start, min(GROUP, rings - start))]
+        direct = z < EARLY
+
+        def forward(part, u=u):
+            for t in (2, 1, 3) if lanes_x == 4 else range(1, lanes_x):
+                remote(part, part, lane_sem.at[u, 0], lane_sem.at[u, 1], {"chan": to_x(t)}).start()
+
+        def sent_back(many, times, u=u):
+            def gone(t, carry):
+                remote(many, many, back_send.at[u], back_recv.at[u, 0], twin).wait_send()
+                return carry
+
+            return functools.partial(lax.fori_loop, 0, times, gone, 0)
+
+        closing.append(sent_back(product_out.at[u, pl.ds(0, rings - 1)], 1))
+        if u:
+            elsewhere = EARLY - jnp.where(direct, 1, 0)
+            closing.append(sent_back(product_out.at[u, 0], elsewhere * (lanes_x - 1)))
+            pl.when(direct)(functools.partial(forward, product_in.at[u, x, 0]))
+        for g, (start, stop) in enumerate(spans):
+            arrived = product_in.at[u, x, pl.ds(start, stop - start)]
             remote(arrived, arrived, back_send.at[u], back_recv.at[u, g], twin).wait_recv()
             begin = start if g else 0
-            part = product_in.at[u, x, pl.ds(begin, min(start + GROUP, rings) - begin)]
-            for t in (2, 1, 3) if lanes_x == 4 else range(1, lanes_x):
-                remote(part, part, lane_sem.at[u, 0], lane_sem.at[u, 1], {"chan": to_x(t)}).start()
+            part = product_in.at[u, x, pl.ds(begin, stop - begin)]
+            if u:
+                pl.when(jnp.logical_not(direct))(functools.partial(forward, part))
+            else:
+                forward(part)
         phase("lwait")
         many = product_in.at[u, pl.ds(0, lanes_x - 1)]
-        lanes_all = remote(many, many, lane_sem.at[u, 0], lane_sem.at[u, 1], twin)
-        lanes_all.wait_recv()
-        closing.append(lanes_all.wait_send)
+        remote(many, many, lane_sem.at[u, 0], lane_sem.at[u, 1], twin).wait_recv()
+
+        def sent_on(count, u=u):
+            many = product_in.at[u, pl.ds(0, lanes_x - 1), pl.ds(0, count)]
+            remote(many, many, lane_sem.at[u, 0], lane_sem.at[u, 1], twin).wait_send()
+
+        one_sent, all_sent = functools.partial(sent_on, 1), functools.partial(sent_on, rings)
+        if u:
+            closing.append(functools.partial(pl.when(direct), one_sent))
+            closing.append(functools.partial(pl.when(jnp.logical_not(direct)), all_sent))
+        else:
+            closing.append(all_sent)
 
         phase("hidden")
         hidden = [
@@ -528,7 +573,7 @@
     rows, cols, depth = prior_pair.shape
     blocks = rows * cols // LANES
     size = rings * blocks
-    groups = -(-(rings - 1) // GROUP)
+    groups = -(-(TAIL - 1) // GROUP) + 1
     vmem = pl.BlockSpec(memory_space=pltpu.VMEM)
     hbm = pl.BlockSpec(memory_space=pltpu.HBM)
     dma = pltpu.SemaphoreType.DMA
@@ -556,7 +601,7 @@
     ]
     return pl.pallas_call(
         functools.partial(kernel, rings, lanes_x),
-        out_shape=jax.ShapeDtypeStruct(prior_pair.shape, BF16),
+        out_shape=pltpu.VMEM(prior_pair.shape, BF16),
         in_specs=[hbm] * len(operands),
         out_specs=vmem,
         scratch_shapes=held

time: 134 us -> 132 us (0.985)
  no operation moved by 1% of the time
where the time goes in v4:
time: 132 us
  Pallas kernels  131 us (99%)
    pallas_call x1, Pallas kernels, body(): pl.pallas_call(functools.partial(kernel, rings, lanes_x), out_shape=pltpu...  131 us

profile of v4, /device:TPU:33, one launch (start us, length us, event | category | flops | bytes accessed | tf_op | source)
XLA Modules:
  0.0 131.6 jit_solution(17894098391392699173)
XLA Ops:
  0.0 130.9 %triangles.1 = bf16[4,256,128]{2,1,0:T(8,128)(2,1)S(1)} custom-call(bf16[4,256,128]{2,1,0:T(8,128)(2,1)} %prior_hbm.1, bf16[4,384]{1,0:T(4,128)(2,1)} %single_hbm.1, s32[4]{0:T(128)} %target_hbm.1, s32[4]{0:T(128)} %mask_hbm.1, f32[1,128]{1,0:T(1,128)} %bitcast.2, f32[1,128]{1,0:T(1,128)} %bitcast.3, bf16[384,128]{1,0:T(8,128)(2,1)} %left_single_hbm.1, ...), custom_call_target="tpu_custom_call" | custom-call | tf_op jit(solution)/shard_map/triangles/pallas_call | solution.py:602
  130.9 0.7 copy.18

commit v5 on v4

--- a/solution.py
+++ b/solution.py
@@ -92,6 +92,7 @@
     tri_out_gain_ref,
     tri_out_ref,
     terms,
+    right_all,
     edges_out,
     edges_in,
     product_out,
@@ -206,9 +207,12 @@
         return [linear[r : r + 1] + picked[r] for r in range(rows)]
 
     right_rows = row_terms(right_single_ref, right_target_ref)
-    mask_rows = [jnp.full((1, depth), mask_of[r], F32) for r in range(rows)]
-    tile = jnp.concatenate(right_rows + mask_rows, axis=0)
-    terms[h, z] = jnp.where(h == 0, tile, pltpu.roll(tile, rows, 0))
+    lane_row = lax.rem(lax.broadcasted_iota(jnp.int32, (1, LANES), 1), rows)
+    mask_row = jnp.zeros((1, LANES), F32)
+    for r in range(rows):
+        mask_row = jnp.where(lane_row == r, mask_of[r], mask_row)
+    for r, row in enumerate(right_rows + [mask_row]):
+        terms[h, z, :, r * LANES : (r + 1) * LANES] = row
 
     phase("barrier")
     pl.semaphore_wait(barrier, q + jnp.minimum(STRIDE, last - q) + 1 + lanes_x - 1)
@@ -363,15 +367,20 @@
     swap(lambda parity: terms.at[parity], 0)
 
     phase("pair")
-    first, second = terms[0], terms[1]
-    upper = lax.broadcasted_iota(jnp.int32, first.shape, 1) < rows
-    right_whole = jnp.where(upper, first, second).reshape(cols, depth)
-    mask_whole = jnp.where(upper, second, first)
-    mask_whole = pltpu.roll(mask_whole, rows, 1).reshape(cols, depth)
+    for parity in range(2):
+        for r in range(rows):
+            part = terms[parity, :, 0, r * LANES : (r + 1) * LANES]
+            right_all[:, parity * rows + r, :] = part
+    right_whole = right_all[...].reshape(cols, depth)
+    lane = lax.broadcasted_iota(jnp.int32, (rings, LANES), 1)
+    source = lax.broadcasted_iota(jnp.int32, (rings, LANES), 0)
+    first, second = (terms[parity, :, 0, rows * LANES :] for parity in range(2))
+    mask_table = jnp.where(lax.rem(lane // rows, 2) == 0, first, second)
     masks = []
     for jh in range(per_row):
         right_t = jnp.transpose(right_whole[jh * LANES : (jh + 1) * LANES])
-        masks.append(jnp.transpose(mask_whole[jh * LANES : (jh + 1) * LANES])[:1])
+        chosen = source == (jh * LANES + lane) // (2 * rows)
+        masks.append(jnp.sum(jnp.where(chosen, mask_table, 0.0), axis=0, keepdims=True))
         for r in range(rows):
             m = r * per_row + jh
             pair[m] = (base[m] + right_t).astype(BF16).astype(F32)
@@ -606,7 +615,8 @@
         out_specs=vmem,
         scratch_shapes=held
         + [
-            pltpu.VMEM((2, rings, 2 * rows, LANES), F32),
+            pltpu.VMEM((2, rings, 1, (rows + 1) * LANES), F32),
+            pltpu.VMEM((rings, 2 * rows, LANES), F32),
             pltpu.VMEM((2, rings, 2, blocks, LANES), BF16),
             pltpu.VMEM((2, 2, rings, 2, blocks, LANES), BF16),
             pltpu.VMEM((2, rings, blocks, LANES), BF16),

time: 132 us -> 128 us (0.970)
  Pallas kernels: 131 us -> 126 us
    pallas_call x1, Pallas kernels: 131 us -> 126 us  [body(): pl.pallas_call(functools.partial(kernel, rings, lanes_x), out_shape=pltpu...]
where the time goes in v5:
time: 128 us; the launch traced here: 127 us
  Pallas kernels  126 us (98%)
    pallas_call x1, Pallas kernels, body(): pl.pallas_call(functools.partial(kernel, rings, lanes_x), out_shape=pltpu...  126 us

profile of v5, /device:TPU:33, one launch (start us, length us, event | category | flops | bytes accessed | tf_op | source)
XLA Modules:
  0.0 126.8 jit_solution(9218919094689988600)
XLA Ops:
  0.0 126.1 %triangles.1 = bf16[4,256,128]{2,1,0:T(8,128)(2,1)S(1)} custom-call(bf16[4,256,128]{2,1,0:T(8,128)(2,1)} %prior_hbm.1, bf16[4,384]{1,0:T(4,128)(2,1)} %single_hbm.1, s32[4]{0:T(128)} %target_hbm.1, s32[4]{0:T(128)} %mask_hbm.1, f32[1,128]{1,0:T(1,128)} %bitcast.2, f32[1,128]{1,0:T(1,128)} %bitcast.3, bf16[384,128]{1,0:T(8,128)(2,1)} %left_single_hbm.1, ...), custom_call_target="tpu_custom_call" | custom-call | tf_op jit(solution)/shard_map/triangles/pallas_call | solution.py:611
  126.1 0.7 copy.18

commit v6 on v5

--- a/solution.py
+++ b/solution.py
@@ -148,7 +148,7 @@
     last = rings - 1
 
     def at(order):
-        return to_z(lax.rem(order + 1, rings))
+        return {"dap": 2 * lax.rem(order + 1, rings) + 1 - h}
 
     def greet(order):
         pl.semaphore_signal(barrier, inc=1, device_id=at(order), device_id_type=MESH)
@@ -237,8 +237,8 @@
     phase("tsend")
 
     def give(source, order):
-        tile = terms.at[h, source]
-        remote(tile, tile, terms_send.at[0], terms_recv.at[source], at(order)).start()
+        tile, landing = terms.at[h, source], terms.at[1 - h, source]
+        remote(tile, landing, terms_send.at[0], terms_recv.at[source], at(order)).start()
 
     def carried(source):
         return lax.rem(source, lanes_x) == x
@@ -367,14 +367,21 @@
     swap(lambda parity: terms.at[parity], 0)
 
     phase("pair")
+    source = lax.broadcasted_iota(jnp.int32, (rings, LANES), 0)
+    order = lax.rem(source + rings - 1, rings)
+    even = lax.rem((q - order - 1 + rings * STRIDE) // STRIDE, 2) == rings % 2
+    same = (order == q) | ((order < q) & jnp.logical_not(even))
+
+    def of_parity(parity, r):
+        got = [terms[core, :, 0, r * LANES : (r + 1) * LANES] for core in range(2)]
+        return jnp.where(same, got[parity], got[1 - parity])
+
     for parity in range(2):
         for r in range(rows):
-            part = terms[parity, :, 0, r * LANES : (r + 1) * LANES]
-            right_all[:, parity * rows + r, :] = part
+            right_all[:, parity * rows + r, :] = of_parity(parity, r)
     right_whole = right_all[...].reshape(cols, depth)
     lane = lax.broadcasted_iota(jnp.int32, (rings, LANES), 1)
-    source = lax.broadcasted_iota(jnp.int32, (rings, LANES), 0)
-    first, second = (terms[parity, :, 0, rows * LANES :] for parity in range(2))
+    first, second = (of_parity(parity, rows) for parity in range(2))
     mask_table = jnp.where(lax.rem(lane // rows, 2) == 0, first, second)
     masks = []
     for jh in range(per_row):

time: 128 us -> 131 us (1.023)
  Pallas kernels: 126 us -> 130 us
    pallas_call x1, Pallas kernels: 126 us -> 130 us  [body(): pl.pallas_call(functools.partial(kernel, rings, lanes_x), out_shape=pltpu...]
where the time goes in v6:
time: 131 us
  Pallas kernels  130 us (99%)
    pallas_call x1, Pallas kernels, body(): pl.pallas_call(functools.partial(kernel, rings, lanes_x), out_shape=pltpu...  130 us

profile of v6, /device:TPU:33, one launch (start us, length us, event | category | flops | bytes accessed | tf_op | source)
XLA Modules:
  0.0 130.9 jit_solution(9378055176209336183)
XLA Ops:
  0.0 130.2 %triangles.1 = bf16[4,256,128]{2,1,0:T(8,128)(2,1)S(1)} custom-call(bf16[4,256,128]{2,1,0:T(8,128)(2,1)} %prior_hbm.1, bf16[4,384]{1,0:T(4,128)(2,1)} %single_hbm.1, s32[4]{0:T(128)} %target_hbm.1, s32[4]{0:T(128)} %mask_hbm.1, f32[1,128]{1,0:T(1,128)} %bitcast.2, f32[1,128]{1,0:T(1,128)} %bitcast.3, bf16[384,128]{1,0:T(8,128)(2,1)} %left_single_hbm.1, ...), custom_call_target="tpu_custom_call" | custom-call | tf_op jit(solution)/shard_map/triangles/pallas_call | solution.py:618
  130.2 0.7 copy.18
